TPU v7x, 32 devices: a whole 2x2x4 slice. The times are simulated.
32 devices in a mesh: samp: 4 (over z), seq: 8 (over y, x, core).
Axes of the slice: x: 2, y: 2, z: 4, core: 2. Of those that a mesh axis runs over, the one named last changes fastest.
Arguments:
- queries: bfloat16 [4, 4096, 3584], P('samp', 'seq'), may hold values from -200 to 200
- keys: bfloat16 [4, 4096, 512], P('samp', 'seq'), may hold values from -6 to 6
- values: bfloat16 [4, 4096, 512], P('samp', 'seq'), may hold values from -6 to 6
- reg_owner: int32 [4], P('samp'), may hold values from 0 to 7
- block_lists: int32 [4, 32, 8], P('samp', 'seq'), may hold values from 0 to 31, as said below
- list_counts: int32 [4, 32], P('samp', 'seq'), may hold values from 0 to 8, as said below
- image_blocks: int32 [4, 32], P('samp', 'seq'), may hold values from 0 to 1, as said below
Outputs:
- attended: bfloat16 [4, 4096, 3584], P('samp', 'seq')
Inputs may be any that keep to these rules, and one draw needn't show every extreme that they name: `block_lists`: block b lies on sequence index b // 4. Entry t of a list is used only where t < the block's count, unused entries are 0. The used entries of one block name blocks of distinct sequence indices other than its own. Over all blocks of one sequence index, at most one distinct block of each other sequence index is named. On the last sequence index of each sample, the lists together name a block of every other index. `list_counts`: 0 for image blocks; at most 8. `image_blocks`: the blocks of the last sequence index of each sample are text blocks.
All inputs are finite; a program needn't handle non-finite values.
Results may differ from a plain program's by a relative error of at most 0.0043.
Values may be sent and summed in bfloat16 or wider, within the bound.
A program may use at most 128 MiB of HBM per device.

v0:
```python
import functools
import math

import jax
import jax.numpy as jnp
from jax import lax
from jax.experimental import pallas as pl
from jax.experimental.pallas import tpu as pltpu
from jax.sharding import PartitionSpec as P

KEY_VALUE_HEADS = 4
HEAD_SIZE = 128
REG = 64
CHUNKS = 8

hidden = -1e30
score_gain = math.log2(math.e) / math.sqrt(HEAD_SIZE)


def stage_list(devices):
    if devices == 8:
        return [(1, 2, 4, 3, 5, 6, 7)]
    rest = list(range(1, devices))
    return [tuple(rest[i : i + 7]) for i in range(0, len(rest), 7)]


def kernel(
    devices,
    lists_ref,
    counts_ref,
    image_ref,
    owner_ref,
    q_hbm,
    k_hbm,
    v_hbm,
    out_ref,
    q_all,
    k_all,
    v_all,
    need_out,
    need_in,
    chunk_out,
    chunk_in,
    reg_out,
    reg_in,
    x_out,
    x_in,
    acc,
    top,
    bias,
    local_sem,
    q_sem,
    send_need,
    recv_need,
    send_chunk,
    recv_chunk,
    send_reg,
    recv_reg,
    send_x,
    recv_x,
):
    me = lax.axis_index("seq")
    blocks, slots = lists_ref.shape
    rows = k_hbm.shape[1]
    heads = q_hbm.shape[1] // HEAD_SIZE
    group = heads // KEY_VALUE_HEADS
    chunk_rows = 2 * REG // CHUNKS
    peers = range(1, devices)

    def peer(k):
        return me ^ k

    barrier = pltpu.get_barrier_semaphore()
    for k in peers:
        pl.semaphore_signal(barrier, inc=1, device_id={"seq": peer(k)})
    k_copy = pltpu.make_async_copy(k_hbm, k_all, local_sem.at[0])
    v_copy = pltpu.make_async_copy(v_hbm, v_all, local_sem.at[1])
    k_copy.start()
    v_copy.start()

    def q_copy(b):
        span = pl.ds(pl.multiple_of(b * rows, rows), rows)
        return pltpu.make_async_copy(q_hbm.at[span], q_all.at[span], q_sem.at[b])

    for b in range(blocks):
        q_copy(b).start()

    lane = lax.broadcasted_iota(jnp.int32, (8, 128), 1)
    wanted = jnp.zeros((8, 128), jnp.int32)
    for b in range(blocks):
        count = counts_ref[b]
        for t in range(slots):
            entry = lists_ref[b, t]
            source = jnp.where(t < count, lax.div(entry, blocks), -1)
            wanted = jnp.where(lane == source, lax.rem(entry, blocks), wanted)
    need_out[...] = wanted
    k_copy.wait()
    v_copy.wait()
    for c in range(CHUNKS):
        whole = k_all if c < CHUNKS // 2 else v_all
        start = (c % (CHUNKS // 2)) * chunk_rows
        chunk_out[c] = whole[0, start : start + chunk_rows]
    pl.semaphore_wait(barrier, devices - 1)

    def need_copy(k):
        return pltpu.make_async_remote_copy(
            need_out, need_in.at[k], send_need.at[k], recv_need.at[k], device_id={"seq": peer(k)}
        )

    def chunk_copy(k):
        return pltpu.make_async_remote_copy(
            chunk_out.at[lax.rem(peer(k), CHUNKS)],
            chunk_in.at[me],
            send_chunk.at[k],
            recv_chunk.at[k],
            device_id={"seq": peer(k)},
        )

    def reg_copy(k):
        return pltpu.make_async_remote_copy(
            reg_out, reg_in.at[me], send_reg.at[k], recv_reg.at[k], device_id={"seq": peer(k)}
        )

    def x_copy(k, g):
        return pltpu.make_async_remote_copy(
            x_out.at[k, g], x_in.at[k, g], send_x.at[k, g], recv_x.at[k, g], device_id={"seq": peer(k)}
        )

    order = list(reversed(peers))
    for k in order:
        need_copy(k).start()
    for k in order:
        chunk_copy(k).start()
    chunk_in[me] = chunk_out[lax.rem(me, CHUNKS)]

    stages = stage_list(devices)

    for k in peers:
        chunk_copy(k).wait_recv()
    mine = chunk_in[owner_ref[0]]
    reg_out[...] = mine
    reg_in[me] = mine
    for k in order:
        reg_copy(k).start()
    for k in peers:
        need_copy(k).wait_recv()
    for group_of in stages:
        for k in group_of:
            row = need_in[k]
            pick = jnp.sum(jnp.where(lane[:1] == me, row[:1], 0))
            k_block = k_all[pick]
            v_block = v_all[pick]
            for g in range(KEY_VALUE_HEADS):
                columns = slice(g * HEAD_SIZE, (g + 1) * HEAD_SIZE)
                x_out[k, g, :rows] = k_block[:, columns]
                x_out[k, g, rows:] = v_block[:, columns]
        for g in range(KEY_VALUE_HEADS):
            for k in group_of:
                x_copy(k, g).start()

    for b in range(blocks):
        count = counts_ref[b]
        for k in peers:
            source = peer(k)
            seen = jnp.int32(0)
            for t in range(slots):
                entry = lists_ref[b, t]
                hit = jnp.logical_and(lax.div(entry, blocks) == source, t < count)
                seen = jnp.where(hit, 1, seen)
            bias[b, k] = jnp.where(seen == 1, 0.0, hidden)

    def attend(b, g, keys, values, masks, first, last):
        index = g * blocks + b
        row_span = pl.ds(pl.multiple_of(b * rows, rows), rows)
        ones = jnp.ones(values.shape, values.dtype)
        wide = jnp.concatenate([values, ones], axis=1)
        columns = [
            pl.ds(pl.multiple_of((g * group + h) * HEAD_SIZE, HEAD_SIZE), HEAD_SIZE)
            for h in range(group)
        ]
        copies = masks.shape[0] // rows
        repeat = keys.shape[0] // 128

        def scored(part):
            query = jnp.concatenate([q_all[row_span, columns[h]] for h in part], axis=0)
            return lax.dot_general(
                query, keys, (((1,), (1,)), ((), ())), preferred_element_type=jnp.float32
            )

        parts = [list(range(group))[i : i + 4] for i in range(0, group, 4)]
        ahead = [scored(part) for part in parts[:1]]
        for step, part in enumerate(parts):
            if step + 1 < len(parts):
                ahead.append(scored(parts[step + 1]))
            scores = ahead[step]
            here = pl.ds(part[0] * rows, len(part) * rows)
            tall = jnp.concatenate([masks] * len(part), axis=0) if copies else masks
            scores = scores * score_gain + tall
            best = jnp.max(scores, axis=1, keepdims=True)
            if first:
                best = jnp.broadcast_to(best, (len(part) * rows, 128))
            else:
                before = top[index, here]
                best = jnp.maximum(before, best)
            spread = jnp.concatenate([best] * repeat, axis=1) if repeat > 1 else best
            weights = jnp.exp2(scores - spread).astype(jnp.bfloat16)
            product = jnp.dot(weights, wide, preferred_element_type=jnp.float32)
            if not first:
                scale = jnp.exp2(before - best)
                product = product + acc[index, here] * jnp.concatenate([scale, scale], axis=1)
            if last:
                merged = product[:, :HEAD_SIZE] / product[:, HEAD_SIZE:]
                merged = merged.astype(out_ref.dtype)
                for n, h in enumerate(part):
                    out_ref[row_span, columns[h]] = merged[n * rows : (n + 1) * rows]
            else:
                acc[index, here] = product
                top[index, here] = best

    def own_step(i, carry):
        b = i // KEY_VALUE_HEADS
        g = lax.rem(i, KEY_VALUE_HEADS)

        @pl.when(g == 0)
        def _():
            q_copy(b).wait()

        column = pl.ds(pl.multiple_of(g * HEAD_SIZE, HEAD_SIZE), HEAD_SIZE)
        below = lax.broadcasted_iota(jnp.int32, (rows, rows), 1) <= lax.broadcasted_iota(
            jnp.int32, (rows, rows), 0
        )
        shut = jnp.where(image_ref[b] == 1, 0.0, hidden)
        masks = jnp.where(below, 0.0, shut)
        attend(b, g, k_all[b, :, column], v_all[b, :, column], masks, True, False)
        return carry

    lax.fori_loop(0, blocks * KEY_VALUE_HEADS, own_step, 0)

    for k in peers:
        reg_copy(k).wait_recv()

    half = CHUNKS // 2

    def far_step(i, carry, stage):
        g = i // blocks
        b = lax.rem(i, blocks)

        @pl.when(b == 0)
        def _():
            for k in stage:
                x_copy(k, g).wait_recv()

        keys = [x_in[k, g, :rows] for k in stage]
        values = [x_in[k, g, rows:] for k in stage]
        masks = [jnp.full((1, rows), bias[b, k]) for k in stage]
        if stage == stages[0]:
            column = pl.ds(pl.multiple_of(g * HEAD_SIZE, HEAD_SIZE), HEAD_SIZE)
            fill = jnp.zeros((128 - REG, HEAD_SIZE), jnp.bfloat16)
            keys += [reg_in[pl.ds(0, half), :, column].reshape(REG, HEAD_SIZE), fill]
            values += [reg_in[pl.ds(half, half), :, column].reshape(REG, HEAD_SIZE), fill]
            side = lax.broadcasted_iota(jnp.int32, (1, 128), 1)
            masks += [jnp.where(side < REG, 0.0, hidden)]
        keys = jnp.concatenate(keys, axis=0)
        values = jnp.concatenate(values, axis=0)
        masks = jnp.concatenate(masks, axis=1)
        attend(b, g, keys, values, masks, False, stage == stages[-1])
        return carry

    for stage in stages:
        lax.fori_loop(
            0, blocks * KEY_VALUE_HEADS, functools.partial(far_step, stage=stage), 0
        )

    for k in peers:
        need_copy(k).wait_send()
        chunk_copy(k).wait_send()
        reg_copy(k).wait_send()
        for g in range(KEY_VALUE_HEADS):
            x_copy(k, g).wait_send()


def per_device(queries, keys, values, reg_owner, block_lists, list_counts, image_blocks):
    devices = lax.axis_size("seq")
    tokens, width = queries.shape[1:]
    kv_width = keys.shape[2]
    blocks = block_lists.shape[1]
    rows = tokens // blocks
    chunk_rows = 2 * REG // CHUNKS
    group_rows = width // kv_width * rows
    bf = jnp.bfloat16
    dma = pltpu.SemaphoreType.DMA
    smem = pl.BlockSpec(memory_space=pltpu.SMEM)
    anywhere = pl.BlockSpec(memory_space=pl.ANY)
    out = pl.pallas_call(
        functools.partial(kernel, devices),
        out_shape=jax.ShapeDtypeStruct((tokens, width), bf),
        in_specs=[smem] * 4 + [anywhere] * 3,
        out_specs=pl.BlockSpec(memory_space=pltpu.VMEM),
        scratch_shapes=[
            pltpu.VMEM((tokens, width), bf),
            pltpu.VMEM((blocks, rows, kv_width), bf),
            pltpu.VMEM((blocks, rows, kv_width), bf),
            pltpu.VMEM((8, 128), jnp.int32),
            pltpu.VMEM((devices, 8, 128), jnp.int32),
            pltpu.VMEM((CHUNKS, chunk_rows, kv_width), bf),
            pltpu.VMEM((devices, chunk_rows, kv_width), bf),
            pltpu.VMEM((chunk_rows, kv_width), bf),
            pltpu.VMEM((devices, chunk_rows, kv_width), bf),
            pltpu.VMEM((devices, KEY_VALUE_HEADS, 2 * rows, HEAD_SIZE), bf),
            pltpu.VMEM((devices, KEY_VALUE_HEADS, 2 * rows, HEAD_SIZE), bf),
            pltpu.VMEM((blocks * KEY_VALUE_HEADS, group_rows, 2 * HEAD_SIZE), jnp.float32),
            pltpu.VMEM((blocks * KEY_VALUE_HEADS, group_rows, 128), jnp.float32),
            pltpu.SMEM((blocks, devices), jnp.float32),
            dma((2,)),
            dma((blocks,)),
            dma((devices,)),
            dma((devices,)),
            dma((devices,)),
            dma((devices,)),
            dma((devices,)),
            dma((devices,)),
            dma((devices, KEY_VALUE_HEADS)),
            dma((devices, KEY_VALUE_HEADS)),
        ],
        compiler_params=pltpu.CompilerParams(
            collective_id=0, has_side_effects=True, vmem_limit_bytes=38 * 1024 * 1024 + devices * kv_width * rows * 8
        ),
    )(
        block_lists[0],
        list_counts[0],
        image_blocks[0],
        reg_owner,
        queries[0],
        keys.reshape(blocks, rows, kv_width),
        values.reshape(blocks, rows, kv_width),
    )
    return out[None]


def solution(mesh):
    placed = (
        P("samp", "seq", None),
        P("samp", "seq", None),
        P("samp", "seq", None),
        P("samp"),
        P("samp", "seq", None),
        P("samp", "seq"),
        P("samp", "seq"),
    )
    return jax.shard_map(
        per_device, mesh=mesh, in_specs=placed, out_specs=P("samp", "seq", None), check_vma=False
    )
```

profile of v0, /device:TPU:1, one launch (start us, length us, event | category | flops | bytes accessed | tf_op | source)
XLA Modules:
  0.0 50.5 jit_solution(3642841241723412777)
XLA Ops:
  0.7 0.0 copy-start
  0.7 2.0 %copy-done = bf16[1,512,3584]{2,1,0:T(8,128)(2,1)S(1)} copy-done((bf16[1,512,3584]{2,1,0:T(8,128)(2,1)S(1)}, bf16[1,512,3584]{2,1,0:T(8,128)(2,1)}, u32[]{:S(2)}) %copy-start) | copy-done | bytes 3670040
  2.7 0.0 copy-start.1
  2.7 1.0 %copy-done.1 = bf16[1,512,512]{2,1,0:T(8,128)(2,1)S(1)} copy-done((bf16[1,512,512]{2,1,0:T(8,128)(2,1)S(1)}, bf16[1,512,512]{2,1,0:T(8,128)(2,1)}, u32[]{:S(2)}) %copy-start.1) | copy-done | bytes 524312
  3.7 0.0 copy-start.2
  3.7 1.0 %copy-done.2 = bf16[1,512,512]{2,1,0:T(8,128)(2,1)S(1)} copy-done((bf16[1,512,512]{2,1,0:T(8,128)(2,1)S(1)}, bf16[1,512,512]{2,1,0:T(8,128)(2,1)}, u32[]{:S(2)}) %copy-start.2) | copy-done | bytes 524312
  4.8 0.0 copy-start.3
  4.8 0.7 %copy-done.3 = s32[1,4,8]{2,1,0:T(4,128)S(1)} copy-done((s32[1,4,8]{2,1,0:T(4,128)S(1)}, s32[1,4,8]{2,1,0:T(4,128)}, u32[]{:S(2)}) %copy-start.3) | copy-done | bytes 152
  5.5 0.0 copy-start.4
  5.5 0.7 %copy-done.4 = s32[1,4]{1,0:T(1,128)S(1)} copy-done((s32[1,4]{1,0:T(1,128)S(1)}, s32[1,4]{1,0:T(1,128)}, u32[]{:S(2)}) %copy-start.4) | copy-done | bytes 40
  6.1 0.0 copy-start.5
  6.1 0.7 %copy-done.5 = s32[1,4]{1,0:T(1,128)S(1)} copy-done((s32[1,4]{1,0:T(1,128)S(1)}, s32[1,4]{1,0:T(1,128)}, u32[]{:S(2)}) %copy-start.5) | copy-done | bytes 40
  6.8 41.9 %shard_map.73 = bf16[512,3584]{1,0:T(8,128)(2,1)S(1)} custom-call(s32[4,8]{1,0:T(4,128)S(1)} %bitcast.11, s32[4]{0:T(128)S(1)} %bitcast.12, s32[4]{0:T(128)S(1)} %bitcast.13, s32[1]{0:T(128)S(6)} %copy.9.owner_ref, bf16[512,3584]{1,0:T(8,128)(2,1)S(1)} %bitcast.8, bf16[4,128,512]{2,1,0:T(8,128)(2,1)S(1)} %bitcast.9, bf16[4,128,512]{2,1,0:T(8,128)(2,1)S(1)} %bitcast.10), custom_call_target="tpu_custom_call" | custom-call | tf_op jit(solution)/shard_map/pallas_call | solution.py:294
  48.7 1.8 %copy.10 = bf16[1,512,3584]{2,1,0:T(8,128)(2,1)} copy(bf16[1,512,3584]{2,1,0:T(8,128)(2,1)S(1)} %bitcast.7) | data formatting | bytes 7340032
Async XLA Ops:
  0.7 2.0 %copy-start = (bf16[1,512,3584]{2,1,0:T(8,128)(2,1)S(1)}, bf16[1,512,3584]{2,1,0:T(8,128)(2,1)}, u32[]{:S(2)}) copy-start(bf16[1,512,3584]{2,1,0:T(8,128)(2,1)} %param.7) | copy-start | bytes 11010052
  2.7 1.0 %copy-start.1 = (bf16[1,512,512]{2,1,0:T(8,128)(2,1)S(1)}, bf16[1,512,512]{2,1,0:T(8,128)(2,1)}, u32[]{:S(2)}) copy-start(bf16[1,512,512]{2,1,0:T(8,128)(2,1)} %param.8) | copy-start | bytes 1572868
  3.7 1.0 %copy-start.2 = (bf16[1,512,512]{2,1,0:T(8,128)(2,1)S(1)}, bf16[1,512,512]{2,1,0:T(8,128)(2,1)}, u32[]{:S(2)}) copy-start(bf16[1,512,512]{2,1,0:T(8,128)(2,1)} %param.9) | copy-start | bytes 1572868
  4.8 0.7 %copy-start.3 = (s32[1,4,8]{2,1,0:T(4,128)S(1)}, s32[1,4,8]{2,1,0:T(4,128)}, u32[]{:S(2)}) copy-start(s32[1,4,8]{2,1,0:T(4,128)} %param.11) | copy-start | bytes 388
  5.5 0.7 %copy-start.4 = (s32[1,4]{1,0:T(1,128)S(1)}, s32[1,4]{1,0:T(1,128)}, u32[]{:S(2)}) copy-start(s32[1,4]{1,0:T(1,128)} %param.12) | copy-start | bytes 52
  6.1 0.7 %copy-start.5 = (s32[1,4]{1,0:T(1,128)S(1)}, s32[1,4]{1,0:T(1,128)}, u32[]{:S(2)}) copy-start(s32[1,4]{1,0:T(1,128)} %param.13) | copy-start | bytes 52
where the time goes:
time: 50.8 us; the launch traced here: 50.5 us
  Pallas kernels  41.9 us (82%)
  local copies, waits for them, and re-layouts  7.94 us (16%)
  between operations  0.67 us (1%)
    pallas_call x1, Pallas kernels, per_device(): pl.pallas_call(functools.partial(kernel, devices), out_shape=jax.ShapeDty...  41.9 us
    unnamed x13, local copies, waits for them, and re-layouts  7.94 us

commit v1 on v0

v1 whole, which is shorter than its diff:
```python
import functools
import math

import jax
import jax.numpy as jnp
from jax import lax
from jax.experimental import pallas as pl
from jax.experimental.pallas import tpu as pltpu
from jax.sharding import PartitionSpec as P

KEY_VALUE_HEADS = 4
HEAD_SIZE = 128
REG = 64
CHUNKS = 8
SUMS = 16
UNITS = 4

hidden = -1e30
score_gain = math.log2(math.e) / math.sqrt(HEAD_SIZE)
bf = jnp.bfloat16
f32 = jnp.float32


def stage_list(devices):
    if devices == 8:
        return [(1, 2, 4, 3, 5, 6, 7)]
    rest = list(range(1, devices))
    return [tuple(rest[i : i + 7]) for i in range(0, len(rest), 7)]


def split(keys):
    scaled = keys.astype(f32) * score_gain
    high = scaled.astype(bf)
    low = (scaled - high.astype(f32)).astype(bf)
    return high, low


def kernel(
    devices,
    lists_hbm,
    counts_hbm,
    image_hbm,
    owner_hbm,
    q_hbm,
    k_hbm,
    v_hbm,
    out_ref,
    lists_ref,
    counts_ref,
    image_ref,
    owner_ref,
    q_all,
    k_all,
    v_all,
    vt_own,
    need_out,
    need_in,
    chunk_out,
    chunk_in,
    reg_out,
    reg_in,
    x_out,
    x_in,
    acc,
    top,
    shown,
    own_mask,
    kk,
    vt,
    s_a,
    s_b,
    small_sem,
    local_sem,
    q_sem,
    send_need,
    recv_need,
    send_chunk,
    recv_chunk,
    send_reg,
    recv_reg,
    send_x,
    recv_x,
):
    me = lax.axis_index("seq")
    blocks, slots = lists_ref.shape
    rows = k_hbm.shape[1]
    heads = q_hbm.shape[1] // HEAD_SIZE
    group = heads // KEY_VALUE_HEADS
    chunk_rows = 2 * REG // CHUNKS
    peers = range(1, devices)
    wide = UNITS * rows
    steps = blocks * group // UNITS

    def peer(k):
        return me ^ k

    small = [
        pltpu.make_async_copy(lists_hbm, lists_ref, small_sem.at[0]),
        pltpu.make_async_copy(counts_hbm, counts_ref, small_sem.at[1]),
        pltpu.make_async_copy(image_hbm, image_ref, small_sem.at[2]),
        pltpu.make_async_copy(owner_hbm, owner_ref, small_sem.at[3]),
    ]
    for copy in small:
        copy.start()
    k_copy = pltpu.make_async_copy(k_hbm, k_all, local_sem.at[0])
    v_copy = pltpu.make_async_copy(v_hbm, v_all, local_sem.at[1])
    k_copy.start()
    v_copy.start()
    barrier = pltpu.get_barrier_semaphore()
    for k in peers:
        pl.semaphore_signal(barrier, inc=1, device_id={"seq": peer(k)})

    def q_copy(b):
        span = pl.ds(pl.multiple_of(b * rows, rows), rows)
        return pltpu.make_async_copy(q_hbm.at[span], q_all.at[span], q_sem.at[b])

    for b in range(blocks):
        q_copy(b).start()

    for copy in small:
        copy.wait()
    lane = lax.broadcasted_iota(jnp.int32, (8, 128), 1)
    wanted = jnp.zeros((8, 128), jnp.int32)
    for b in range(blocks):
        count = counts_ref[b]
        for t in range(slots):
            entry = lists_ref[b, t]
            source = jnp.where(t < count, lax.div(entry, blocks), -1)
            wanted = jnp.where(lane == source, lax.rem(entry, blocks), wanted)
    need_out[...] = wanted
    k_copy.wait()
    v_copy.wait()
    for c in range(CHUNKS):
        whole = k_all if c < CHUNKS // 2 else v_all
        start = (c % (CHUNKS // 2)) * chunk_rows
        chunk_out[c] = whole[0, start : start + chunk_rows]
    pl.semaphore_wait(barrier, devices - 1)

    def need_copy(k):
        return pltpu.make_async_remote_copy(
            need_out, need_in.at[k], send_need.at[k], recv_need.at[k], device_id={"seq": peer(k)}
        )

    def chunk_copy(k):
        return pltpu.make_async_remote_copy(
            chunk_out.at[lax.rem(peer(k), CHUNKS)],
            chunk_in.at[me],
            send_chunk.at[k],
            recv_chunk.at[k],
            device_id={"seq": peer(k)},
        )

    def reg_copy(k):
        return pltpu.make_async_remote_copy(
            reg_out, reg_in.at[me], send_reg.at[k], recv_reg.at[k], device_id={"seq": peer(k)}
        )

    def x_copy(k, g):
        return pltpu.make_async_remote_copy(
            x_out.at[k, g], x_in.at[k, g], send_x.at[k, g], recv_x.at[k, g], device_id={"seq": peer(k)}
        )

    order = list(reversed(peers))
    for k in order:
        need_copy(k).start()
    for k in order:
        chunk_copy(k).start()
    chunk_in[me] = chunk_out[lax.rem(me, CHUNKS)]

    for b in range(blocks):
        for g in range(KEY_VALUE_HEADS):
            column = slice(g * HEAD_SIZE, (g + 1) * HEAD_SIZE)
            vt_own[b, g, :HEAD_SIZE] = v_all[b, :, column].T
            vt_own[b, g, HEAD_SIZE:] = jnp.ones((SUMS, rows), bf)

    stages = stage_list(devices)

    for k in peers:
        need_copy(k).wait_recv()
    for group_of in stages:
        for k in group_of:
            row = need_in[k]
            pick = jnp.sum(jnp.where(lane[:1] == me, row[:1], 0))
            for g in range(KEY_VALUE_HEADS):
                columns = slice(g * HEAD_SIZE, (g + 1) * HEAD_SIZE)
                x_out[k, g, :rows] = k_all[pick, :, columns]
                x_out[k, g, rows:] = vt_own[pick, g, :HEAD_SIZE]
            x_copy(k, 0).start()
    for k in peers:
        chunk_copy(k).wait_recv()
    mine = chunk_in[owner_ref[0]]
    reg_out[...] = mine
    reg_in[me] = mine
    for k in order:
        reg_copy(k).start()
    for group_of in stages:
        for g in range(1, KEY_VALUE_HEADS):
            for k in group_of:
                x_copy(k, g).start()

    for k in peers:
        source = peer(k)
        for b in range(blocks):
            count = counts_ref[b]
            seen = jnp.int32(0)
            for t in range(slots):
                entry = lists_ref[b, t]
                hit = jnp.logical_and(lax.div(entry, blocks) == source, t < count)
                seen = jnp.where(hit, 1, seen)
            value = jnp.where(seen == 1, 0.0, hidden)
            shown[k, :, b * group * rows : (b + 1) * group * rows] = jnp.full((8, group * rows), value)

    key_side = lax.broadcasted_iota(jnp.int32, (rows, rows), 0)
    row_side = lax.broadcasted_iota(jnp.int32, (rows, rows), 1)
    for b in range(blocks):
        shut = jnp.where(image_ref[b] == 1, 0.0, hidden)
        own_mask[b] = jnp.where(key_side <= row_side, 0.0, shut)
    vt[HEAD_SIZE:] = jnp.ones((SUMS, vt.shape[1]), bf)

    nt = (((1,), (1,)), ((), ()))

    def own_step(i, carry):
        b = i // KEY_VALUE_HEADS
        g = lax.rem(i, KEY_VALUE_HEADS)

        @pl.when(g == 0)
        def _():
            q_copy(b).wait()

        column = pl.ds(pl.multiple_of(g * HEAD_SIZE, HEAD_SIZE), HEAD_SIZE)
        row_span = pl.ds(pl.multiple_of(b * rows, rows), rows)
        high, low = split(k_all[b, :, column])
        both = jnp.concatenate([high, low], axis=1)
        mask = own_mask[b]
        query = jnp.concatenate(
            [
                q_all[row_span, pl.ds(pl.multiple_of((g * group + h) * HEAD_SIZE, HEAD_SIZE), HEAD_SIZE)]
                for h in range(group)
            ],
            axis=0,
        )
        query = jnp.concatenate([query, query], axis=1)
        scores = lax.dot_general(both, query, nt, preferred_element_type=f32)
        scores = scores + jnp.concatenate([mask] * group, axis=1)
        best = jnp.max(scores, axis=0, keepdims=True)
        weights = jnp.exp2(scores - best).astype(bf)
        product = jnp.dot(vt_own[b, g], weights, preferred_element_type=f32)
        place = pl.ds(pl.multiple_of(b * group * rows, rows), group * rows)
        acc[g, :, place] = product[: HEAD_SIZE + 8]
        top[g, :, place] = jnp.broadcast_to(best, (8, group * rows))
        return carry

    lax.fori_loop(0, blocks * KEY_VALUE_HEADS, own_step, 0)

    for k in peers:
        reg_copy(k).wait_recv()

    half = CHUNKS // 2

    def far_group(g, carry, stage):
        first, last = stage == stages[0], stage == stages[-1]
        total = len(stage) * rows + (REG if first else 0)
        for k in stage:
            x_copy(k, g).wait_recv()
        for n, k in enumerate(stage):
            high, low = split(x_in[k, g, :rows])
            kk[n * rows : (n + 1) * rows, :HEAD_SIZE] = high
            kk[n * rows : (n + 1) * rows, HEAD_SIZE:] = low
            vt[:HEAD_SIZE, n * rows : (n + 1) * rows] = x_in[k, g, rows:]
        if first:
            column = pl.ds(pl.multiple_of(g * HEAD_SIZE, HEAD_SIZE), HEAD_SIZE)
            begin = len(stage) * rows
            high, low = split(reg_in[pl.ds(0, half), :, column].reshape(REG, HEAD_SIZE))
            kk[begin : begin + REG, :HEAD_SIZE] = high
            kk[begin : begin + REG, HEAD_SIZE:] = low
            vt[:HEAD_SIZE, begin : begin + REG] = reg_in[pl.ds(half, half), :, column].reshape(REG, HEAD_SIZE).T

        def unit(j, n):
            u = j * UNITS + n
            b = lax.div(u, group)
            h = lax.rem(u, group)
            row_span = pl.ds(pl.multiple_of(b * rows, rows), rows)
            column = pl.ds(pl.multiple_of((g * group + h) * HEAD_SIZE, HEAD_SIZE), HEAD_SIZE)
            return row_span, column

        def score(j, s_ref):
            query = jnp.concatenate([q_all[unit(j, n)] for n in range(UNITS)], axis=0)
            query = jnp.concatenate([query, query], axis=1)
            s_ref[:total] = lax.dot_general(kk[:total], query, nt, preferred_element_type=f32)

        def merge(j, s_ref):
            place = pl.ds(pl.multiple_of(j * wide, wide), wide)
            before = top[g, :, place]
            best = before
            for n, k in enumerate(stage):
                block = s_ref[n * rows : (n + 1) * rows].reshape(rows // 8, 8, wide)
                best = jnp.maximum(best, jnp.max(block, axis=0) + shown[k, :, place])
            if first:
                block = s_ref[len(stage) * rows : total].reshape(REG // 8, 8, wide)
                best = jnp.maximum(best, jnp.max(block, axis=0))
            best = jnp.broadcast_to(jnp.max(best, axis=0, keepdims=True), (8, wide))
            parts = []
            for n, k in enumerate(stage):
                shift = shown[k, :, place] - best
                block = s_ref[n * rows : (n + 1) * rows].reshape(rows // 8, 8, wide)
                parts.append(jnp.exp2(block + shift[None]).reshape(rows, wide).astype(bf))
            if first:
                block = s_ref[len(stage) * rows : total].reshape(REG // 8, 8, wide)
                parts.append(jnp.exp2(block - best[None]).reshape(REG, wide).astype(bf))
            weights = jnp.concatenate(parts, axis=0)
            product = jnp.dot(vt[:, :total], weights, preferred_element_type=f32)[: HEAD_SIZE + 8]
            scale = jnp.exp2(before - best)
            product = product.reshape(HEAD_SIZE // 8 + 1, 8, wide)
            product = product + acc[g, :, place].reshape(HEAD_SIZE // 8 + 1, 8, wide) * scale[None]
            if last:
                share = 1.0 / product[HEAD_SIZE // 8]
                merged = (product[: HEAD_SIZE // 8] * share[None]).reshape(HEAD_SIZE, wide)
                for n in range(UNITS):
                    one = merged[:, n * rows : (n + 1) * rows].T
                    out_ref[unit(j, n)] = one.astype(out_ref.dtype)
            else:
                acc[g, :, place] = product.reshape(HEAD_SIZE + 8, wide)
                top[g, :, place] = best

        score(0, s_a)

        def pair(i, carry):
            score(2 * i + 1, s_b)
            merge(2 * i, s_a)
            score(2 * i + 2, s_a)
            merge(2 * i + 1, s_b)
            return carry

        pairs = (steps - 1) // 2
        lax.fori_loop(0, pairs, pair, 0)
        if steps % 2 == 0:
            score(steps - 1, s_b)
            merge(steps - 2, s_a)
            merge(steps - 1, s_b)
        else:
            merge(steps - 1, s_a)
        return carry

    for stage in stages:
        lax.fori_loop(0, KEY_VALUE_HEADS, functools.partial(far_group, stage=stage), 0)

    for k in peers:
        need_copy(k).wait_send()
        chunk_copy(k).wait_send()
        reg_copy(k).wait_send()
        for g in range(KEY_VALUE_HEADS):
            x_copy(k, g).wait_send()


def per_device(queries, keys, values, reg_owner, block_lists, list_counts, image_blocks):
    devices = lax.axis_size("seq")
    tokens, width = queries.shape[1:]
    kv_width = keys.shape[2]
    blocks, slots = block_lists.shape[1:]
    rows = tokens // blocks
    chunk_rows = 2 * REG // CHUNKS
    spread = width // kv_width * tokens
    far = max(len(stage) for stage in stage_list(devices)) * rows + REG
    dma = pltpu.SemaphoreType.DMA
    pinned = functools.partial(pltpu.with_memory_space_constraint, memory_space=pltpu.HBM)
    anywhere = pl.BlockSpec(memory_space=pltpu.HBM)
    out = pl.pallas_call(
        functools.partial(kernel, devices),
        out_shape=jax.ShapeDtypeStruct((tokens, width), bf),
        in_specs=[anywhere] * 7,
        out_specs=pl.BlockSpec(memory_space=pltpu.VMEM),
        scratch_shapes=[
            pltpu.SMEM((blocks, slots), jnp.int32),
            pltpu.SMEM((blocks,), jnp.int32),
            pltpu.SMEM((blocks,), jnp.int32),
            pltpu.SMEM((1,), jnp.int32),
            pltpu.VMEM((tokens, width), bf),
            pltpu.VMEM((blocks, rows, kv_width), bf),
            pltpu.VMEM((blocks, rows, kv_width), bf),
            pltpu.VMEM((blocks, KEY_VALUE_HEADS, HEAD_SIZE + SUMS, rows), bf),
            pltpu.VMEM((8, 128), jnp.int32),
            pltpu.VMEM((devices, 8, 128), jnp.int32),
            pltpu.VMEM((CHUNKS, chunk_rows, kv_width), bf),
            pltpu.VMEM((devices, chunk_rows, kv_width), bf),
            pltpu.VMEM((chunk_rows, kv_width), bf),
            pltpu.VMEM((devices, chunk_rows, kv_width), bf),
            pltpu.VMEM((devices, KEY_VALUE_HEADS, 2 * rows, HEAD_SIZE), bf),
            pltpu.VMEM((devices, KEY_VALUE_HEADS, 2 * rows, HEAD_SIZE), bf),
            pltpu.VMEM((KEY_VALUE_HEADS, HEAD_SIZE + 8, spread), f32),
            pltpu.VMEM((KEY_VALUE_HEADS, 8, spread), f32),
            pltpu.VMEM((devices, 8, spread), f32),
            pltpu.VMEM((blocks, rows, rows), f32),
            pltpu.VMEM((far, 2 * HEAD_SIZE), bf),
            pltpu.VMEM((HEAD_SIZE + SUMS, far), bf),
            pltpu.VMEM((far, UNITS * rows), f32),
            pltpu.VMEM((far, UNITS * rows), f32),
            dma((4,)),
            dma((2,)),
            dma((blocks,)),
            dma((devices,)),
            dma((devices,)),
            dma((devices,)),
            dma((devices,)),
            dma((devices,)),
            dma((devices,)),
            dma((devices, KEY_VALUE_HEADS)),
            dma((devices, KEY_VALUE_HEADS)),
        ],
        compiler_params=pltpu.CompilerParams(
            collective_id=0, has_side_effects=True, vmem_limit_bytes=42 * 1024 * 1024 + devices * kv_width * rows * 4
        ),
    )(
        pinned(block_lists[0]),
        pinned(list_counts[0]),
        pinned(image_blocks[0]),
        reg_owner,
        pinned(queries[0]),
        pinned(keys.reshape(blocks, rows, kv_width)),
        pinned(values.reshape(blocks, rows, kv_width)),
    )
    return out[None]


def solution(mesh):
    placed = (
        P("samp", "seq", None),
        P("samp", "seq", None),
        P("samp", "seq", None),
        P("samp"),
        P("samp", "seq", None),
        P("samp", "seq"),
        P("samp", "seq"),
    )
    return jax.shard_map(
        per_device, mesh=mesh, in_specs=placed, out_specs=P("samp", "seq", None), check_vma=False
    )
```

time: 50.8 us -> 44 us (0.87)
  local copies, waits for them, and re-layouts: 7.94 us -> 1.84 us
  Pallas kernels: 41.9 us -> 41.1 us
    unnamed x13 -> x1, local copies, waits for them, and re-layouts: 7.94 us -> 1.84 us
    pallas_call x1, Pallas kernels: 41.9 us -> 41.1 us  [per_device(): pl.pallas_call(functools.partial(kernel, devices), out_shape=jax.ShapeDty...]
where the time goes in v1:
time: 44 us; the launch traced here: 43.6 us
  Pallas kernels  41.1 us (93%)
  local copies, waits for them, and re-layouts  1.84 us (4%)
  between operations  0.66 us (2%)
    pallas_call x1, Pallas kernels, per_device(): pl.pallas_call(functools.partial(kernel, devices), out_shape=jax.ShapeDty...  41.1 us
    unnamed x1, local copies, waits for them, and re-layouts  1.84 us

profile of v1, /device:TPU:1, one launch (start us, length us, event | category | flops | bytes accessed | tf_op | source)
XLA Modules:
  0.0 43.6 jit_solution(13288560988925361369)
XLA Ops:
  0.7 41.1 %shard_map.73 = bf16[512,3584]{1,0:T(8,128)(2,1)S(1)} custom-call(s32[4,8]{1,0:T(4,128)} %bitcast.11, s32[4]{0:T(128)} %bitcast.12, s32[4]{0:T(128)} %bitcast.13, s32[1]{0:T(128)S(6)} %copy.9.owner_hbm, bf16[512,3584]{1,0:T(8,128)(2,1)} %bitcast.8, bf16[4,128,512]{2,1,0:T(8,128)(2,1)} %bitcast.9, bf16[4,128,512]{2,1,0:T(8,128)(2,1)} %bitcast.10), custom_call_target="tpu_custom_call" | custom-call | tf_op jit(solution)/shard_map/pallas_call | solution.py:367
  41.8 1.8 %copy.10 = bf16[1,512,3584]{2,1,0:T(8,128)(2,1)} copy(bf16[1,512,3584]{2,1,0:T(8,128)(2,1)S(1)} %bitcast.7) | data formatting | bytes 7340032

commit v2 on v1

--- a/solution.py
+++ b/solution.py
@@ -26,6 +26,18 @@
         return [(1, 2, 4, 3, 5, 6, 7)]
     rest = list(range(1, devices))
     return [tuple(rest[i : i + 7]) for i in range(0, len(rest), 7)]
+
+
+def last_list(devices):
+    if devices == 8:
+        return [(1, 2, 4, 3, 5), (6, 7)]
+    return stage_list(devices)
+
+
+def part_of(entry, blocks):
+    if blocks & (blocks - 1):
+        return lax.div(entry, blocks), lax.rem(entry, blocks)
+    return lax.shift_right_logical(entry, blocks.bit_length() - 1), lax.bitwise_and(entry, blocks - 1)
 
 
 def split(keys):
@@ -69,6 +81,8 @@
     vt,
     s_a,
     s_b,
+    m_a,
+    m_b,
     small_sem,
     local_sem,
     q_sem,
@@ -121,12 +135,15 @@
         copy.wait()
     lane = lax.broadcasted_iota(jnp.int32, (8, 128), 1)
     wanted = jnp.zeros((8, 128), jnp.int32)
+    sources = []
     for b in range(blocks):
         count = counts_ref[b]
+        sources.append([])
         for t in range(slots):
-            entry = lists_ref[b, t]
-            source = jnp.where(t < count, lax.div(entry, blocks), -1)
-            wanted = jnp.where(lane == source, lax.rem(entry, blocks), wanted)
+            source, local = part_of(lists_ref[b, t], blocks)
+            source = jnp.where(t < count, source, -1)
+            sources[b].append(source)
+            wanted = jnp.where(lane == source, local, wanted)
     need_out[...] = wanted
     k_copy.wait()
     v_copy.wait()
@@ -177,14 +194,19 @@
 
     for k in peers:
         need_copy(k).wait_recv()
+    picks = {}
+    for k in peers:
+        row = need_in[k]
+        picks[k] = jnp.sum(jnp.where(lane[:1] == me, row[:1], 0))
+
+    def fill(k, g):
+        columns = slice(g * HEAD_SIZE, (g + 1) * HEAD_SIZE)
+        x_out[k, g, :rows] = k_all[picks[k], :, columns]
+        x_out[k, g, rows:] = vt_own[picks[k], g, :HEAD_SIZE]
+
     for group_of in stages:
         for k in group_of:
-            row = need_in[k]
-            pick = jnp.sum(jnp.where(lane[:1] == me, row[:1], 0))
-            for g in range(KEY_VALUE_HEADS):
-                columns = slice(g * HEAD_SIZE, (g + 1) * HEAD_SIZE)
-                x_out[k, g, :rows] = k_all[pick, :, columns]
-                x_out[k, g, rows:] = vt_own[pick, g, :HEAD_SIZE]
+            fill(k, 0)
             x_copy(k, 0).start()
     for k in peers:
         chunk_copy(k).wait_recv()
@@ -193,21 +215,17 @@
     reg_in[me] = mine
     for k in order:
         reg_copy(k).start()
-    for group_of in stages:
-        for g in range(1, KEY_VALUE_HEADS):
+    for g in range(1, KEY_VALUE_HEADS):
+        for group_of in stages:
             for k in group_of:
+                fill(k, g)
                 x_copy(k, g).start()
 
     for k in peers:
         source = peer(k)
         for b in range(blocks):
-            count = counts_ref[b]
-            seen = jnp.int32(0)
-            for t in range(slots):
-                entry = lists_ref[b, t]
-                hit = jnp.logical_and(lax.div(entry, blocks) == source, t < count)
-                seen = jnp.where(hit, 1, seen)
-            value = jnp.where(seen == 1, 0.0, hidden)
+            seen = functools.reduce(jnp.logical_or, [found == source for found in sources[b]])
+            value = jnp.where(seen, 0.0, hidden)
             shown[k, :, b * group * rows : (b + 1) * group * rows] = jnp.full((8, group * rows), value)
 
     key_side = lax.broadcasted_iota(jnp.int32, (rows, rows), 0)
@@ -219,46 +237,45 @@
 
     nt = (((1,), (1,)), ((), ()))
 
-    def own_step(i, carry):
-        b = i // KEY_VALUE_HEADS
-        g = lax.rem(i, KEY_VALUE_HEADS)
-
-        @pl.when(g == 0)
-        def _():
-            q_copy(b).wait()
-
-        column = pl.ds(pl.multiple_of(g * HEAD_SIZE, HEAD_SIZE), HEAD_SIZE)
+    def own_step(b, carry):
+        q_copy(b).wait()
         row_span = pl.ds(pl.multiple_of(b * rows, rows), rows)
-        high, low = split(k_all[b, :, column])
-        both = jnp.concatenate([high, low], axis=1)
-        mask = own_mask[b]
-        query = jnp.concatenate(
-            [
-                q_all[row_span, pl.ds(pl.multiple_of((g * group + h) * HEAD_SIZE, HEAD_SIZE), HEAD_SIZE)]
-                for h in range(group)
-            ],
-            axis=0,
-        )
-        query = jnp.concatenate([query, query], axis=1)
-        scores = lax.dot_general(both, query, nt, preferred_element_type=f32)
-        scores = scores + jnp.concatenate([mask] * group, axis=1)
-        best = jnp.max(scores, axis=0, keepdims=True)
-        weights = jnp.exp2(scores - best).astype(bf)
-        product = jnp.dot(vt_own[b, g], weights, preferred_element_type=f32)
         place = pl.ds(pl.multiple_of(b * group * rows, rows), group * rows)
-        acc[g, :, place] = product[: HEAD_SIZE + 8]
-        top[g, :, place] = jnp.broadcast_to(best, (8, group * rows))
+        mask = jnp.concatenate([own_mask[b]] * group, axis=1)
+
+        def scored(g):
+            high, low = split(k_all[b, :, g * HEAD_SIZE : (g + 1) * HEAD_SIZE])
+            both = jnp.concatenate([high, low], axis=1)
+            query = jnp.concatenate(
+                [
+                    q_all[row_span, (g * group + h) * HEAD_SIZE : (g * group + h + 1) * HEAD_SIZE]
+                    for h in range(group)
+                ],
+                axis=0,
+            )
+            query = jnp.concatenate([query, query], axis=1)
+            return lax.dot_general(both, query, nt, preferred_element_type=f32) + mask
+
+        ahead = scored(0)
+        for g in range(KEY_VALUE_HEADS):
+            scores = ahead
+            if g + 1 < KEY_VALUE_HEADS:
+                ahead = scored(g + 1)
+            best = jnp.max(scores, axis=0, keepdims=True)
+            weights = jnp.exp2(scores - best).astype(bf)
+            product = jnp.dot(vt_own[b, g], weights, preferred_element_type=f32)
+            acc[g, :, place] = product[: HEAD_SIZE + 8]
+            top[g, :, place] = jnp.broadcast_to(best, (8, group * rows))
         return carry
 
-    lax.fori_loop(0, blocks * KEY_VALUE_HEADS, own_step, 0)
+    lax.fori_loop(0, blocks, own_step, 0)
 
     for k in peers:
         reg_copy(k).wait_recv()
 
     half = CHUNKS // 2
 
-    def far_group(g, carry, stage):
-        first, last = stage == stages[0], stage == stages[-1]
+    def far_stage(g, stage, first, last):
         total = len(stage) * rows + (REG if first else 0)
         for k in stage:
             x_copy(k, g).wait_recv()
@@ -275,74 +292,77 @@
             kk[begin : begin + REG, HEAD_SIZE:] = low
             vt[:HEAD_SIZE, begin : begin + REG] = reg_in[pl.ds(half, half), :, column].reshape(REG, HEAD_SIZE).T
 
+        pieces = [(n * rows, rows, k) for n, k in enumerate(stage)]
+        if first:
+            pieces.append((len(stage) * rows, REG, None))
+
         def unit(j, n):
             u = j * UNITS + n
-            b = lax.div(u, group)
-            h = lax.rem(u, group)
-            row_span = pl.ds(pl.multiple_of(b * rows, rows), rows)
+            b, h = u // group, u % group
             column = pl.ds(pl.multiple_of((g * group + h) * HEAD_SIZE, HEAD_SIZE), HEAD_SIZE)
-            return row_span, column
-
-        def score(j, s_ref):
+            return pl.ds(b * rows, rows), column
+
+        def place_of(j):
+            return pl.ds(j * wide, wide)
+
+        def score(j, s_ref, m_ref):
+            place = place_of(j)
             query = jnp.concatenate([q_all[unit(j, n)] for n in range(UNITS)], axis=0)
             query = jnp.concatenate([query, query], axis=1)
-            s_ref[:total] = lax.dot_general(kk[:total], query, nt, preferred_element_type=f32)
-
-        def merge(j, s_ref):
-            place = pl.ds(pl.multiple_of(j * wide, wide), wide)
+            scores = lax.dot_general(kk[:total], query, nt, preferred_element_type=f32)
+            s_ref[:total] = scores
+            best = top[g, :, place]
+            for begin, size, k in pieces:
+                block = jnp.max(scores[begin : begin + size].reshape(size // 8, 8, wide), axis=0)
+                best = jnp.maximum(best, block if k is None else block + shown[k, :, place])
+            m_ref[...] = jnp.broadcast_to(jnp.max(best, axis=0, keepdims=True), (8, wide))
+
+        def merge(j, s_ref, m_ref):
+            place = place_of(j)
             before = top[g, :, place]
-            best = before
-            for n, k in enumerate(stage):
-                block = s_ref[n * rows : (n + 1) * rows].reshape(rows // 8, 8, wide)
-                best = jnp.maximum(best, jnp.max(block, axis=0) + shown[k, :, place])
-            if first:
-                block = s_ref[len(stage) * rows : total].reshape(REG // 8, 8, wide)
-                best = jnp.maximum(best, jnp.max(block, axis=0))
-            best = jnp.broadcast_to(jnp.max(best, axis=0, keepdims=True), (8, wide))
-            parts = []
-            for n, k in enumerate(stage):
-                shift = shown[k, :, place] - best
-                block = s_ref[n * rows : (n + 1) * rows].reshape(rows // 8, 8, wide)
-                parts.append(jnp.exp2(block + shift[None]).reshape(rows, wide).astype(bf))
-            if first:
-                block = s_ref[len(stage) * rows : total].reshape(REG // 8, 8, wide)
-                parts.append(jnp.exp2(block - best[None]).reshape(REG, wide).astype(bf))
-            weights = jnp.concatenate(parts, axis=0)
-            product = jnp.dot(vt[:, :total], weights, preferred_element_type=f32)[: HEAD_SIZE + 8]
+            best = m_ref[...]
+            product = None
+            for c in range(0, len(pieces), 2):
+                parts = []
+                for begin, size, k in pieces[c : c + 2]:
+                    shift = -best if k is None else shown[k, :, place] - best
+                    block = s_ref[begin : begin + size].reshape(size // 8, 8, wide)
+                    parts.append(jnp.exp2(block + shift[None]).reshape(size, wide).astype(bf))
+                begin = pieces[c][0]
+                weights = jnp.concatenate(parts, axis=0)
+                more = jnp.dot(vt[:, begin : begin + weights.shape[0]], weights, preferred_element_type=f32)
+                product = more if product is None else product + more
+            product = product[: HEAD_SIZE + 8]
             scale = jnp.exp2(before - best)
             product = product.reshape(HEAD_SIZE // 8 + 1, 8, wide)
             product = product + acc[g, :, place].reshape(HEAD_SIZE // 8 + 1, 8, wide) * scale[None]
             if last:
                 share = 1.0 / product[HEAD_SIZE // 8]
-                merged = (product[: HEAD_SIZE // 8] * share[None]).reshape(HEAD_SIZE, wide)
+                merged = (product[: HEAD_SIZE // 8] * share[None]).reshape(HEAD_SIZE, wide).astype(bf)
                 for n in range(UNITS):
-                    one = merged[:, n * rows : (n + 1) * rows].T
-                    out_ref[unit(j, n)] = one.astype(out_ref.dtype)
+                    out_ref[unit(j, n)] = merged[:, n * rows : (n + 1) * rows].T
             else:
                 acc[g, :, place] = product.reshape(HEAD_SIZE + 8, wide)
                 top[g, :, place] = best
 
-        score(0, s_a)
-
-        def pair(i, carry):
-            score(2 * i + 1, s_b)
-            merge(2 * i, s_a)
-            score(2 * i + 2, s_a)
-            merge(2 * i + 1, s_b)
-            return carry
-
-        pairs = (steps - 1) // 2
-        lax.fori_loop(0, pairs, pair, 0)
-        if steps % 2 == 0:
-            score(steps - 1, s_b)
-            merge(steps - 2, s_a)
-            merge(steps - 1, s_b)
-        else:
-            merge(steps - 1, s_a)
+        score(0, s_a, m_a)
+
+        buffers = ((s_a, m_a), (s_b, m_b))
+        for j in range(steps):
+            if j + 1 < steps:
+                score(j + 1, *buffers[(j + 1) % 2])
+            merge(j, *buffers[j % 2])
+
+    def far_group(g, carry, plan):
+        for stage in plan:
+            far_stage(g, stage, stage == plan[0], stage == plan[-1])
         return carry
 
-    for stage in stages:
-        lax.fori_loop(0, KEY_VALUE_HEADS, functools.partial(far_group, stage=stage), 0)
+    ends = last_list(devices)
+    same = KEY_VALUE_HEADS - (ends != stages)
+    lax.fori_loop(0, same, functools.partial(far_group, plan=stages), 0)
+    for g in range(same, KEY_VALUE_HEADS):
+        far_group(g, 0, ends)
 
     for k in peers:
         need_copy(k).wait_send()
@@ -394,6 +414,8 @@
             pltpu.VMEM((HEAD_SIZE + SUMS, far), bf),
             pltpu.VMEM((far, UNITS * rows), f32),
             pltpu.VMEM((far, UNITS * rows), f32),
+            pltpu.VMEM((8, UNITS * rows), f32),
+            pltpu.VMEM((8, UNITS * rows), f32),
             dma((4,)),
             dma((2,)),
             dma((blocks,)),

time: 44 us -> 40.7 us (0.925)
  Pallas kernels: 41.1 us -> 38.1 us
    pallas_call x1, Pallas kernels: 41.1 us -> 38.1 us  [per_device(): pl.pallas_call(functools.partial(kernel, devices), out_shape=jax.ShapeDty...]
where the time goes in v2:
time: 40.7 us; the launch traced here: 40.5 us
  Pallas kernels  38.1 us (94%)
  local copies, waits for them, and re-layouts  1.84 us (5%)
  between operations  0.66 us (2%)
    pallas_call x1, Pallas kernels, per_device(): pl.pallas_call(functools.partial(kernel, devices), out_shape=jax.ShapeDty...  38.1 us
    unnamed x1, local copies, waits for them, and re-layouts  1.84 us

profile of v2, /device:TPU:1, one launch (start us, length us, event | category | flops | bytes accessed | tf_op | source)
XLA Modules:
  0.0 40.5 jit_solution(1201429518072412660)
XLA Ops:
  0.7 38.1 %shard_map.73 = bf16[512,3584]{1,0:T(8,128)(2,1)S(1)} custom-call(s32[4,8]{1,0:T(4,128)} %bitcast.11, s32[4]{0:T(128)} %bitcast.12, s32[4]{0:T(128)} %bitcast.13, s32[1]{0:T(128)S(6)} %copy.9.owner_hbm, bf16[512,3584]{1,0:T(8,128)(2,1)} %bitcast.8, bf16[4,128,512]{2,1,0:T(8,128)(2,1)} %bitcast.9, bf16[4,128,512]{2,1,0:T(8,128)(2,1)} %bitcast.10), custom_call_target="tpu_custom_call" | custom-call | tf_op jit(solution)/shard_map/pallas_call | solution.py:387
  38.7 1.8 %copy.10 = bf16[1,512,3584]{2,1,0:T(8,128)(2,1)} copy(bf16[1,512,3584]{2,1,0:T(8,128)(2,1)S(1)} %bitcast.7) | data formatting | bytes 7340032

commit v3 on v2

--- a/solution.py
+++ b/solution.py
@@ -23,15 +23,13 @@
 
 def stage_list(devices):
     if devices == 8:
-        return [(1, 2, 4, 3, 5, 6, 7)]
+        return [(1, 2, 4, 3, 5), (6, 7)]
     rest = list(range(1, devices))
     return [tuple(rest[i : i + 7]) for i in range(0, len(rest), 7)]
 
 
-def last_list(devices):
-    if devices == 8:
-        return [(1, 2, 4, 3, 5), (6, 7)]
-    return stage_list(devices)
+def late_peers(devices):
+    return stage_list(devices)[-1] if devices == 8 else ()
 
 
 def part_of(entry, blocks):
@@ -83,16 +81,16 @@
     s_b,
     m_a,
     m_b,
+    held,
+    held_top,
+    out_all,
+    out_sem,
     small_sem,
     local_sem,
     q_sem,
-    send_need,
+    send_sem,
     recv_need,
-    send_chunk,
-    recv_chunk,
-    send_reg,
-    recv_reg,
-    send_x,
+    recv_sem,
     recv_x,
 ):
     me = lax.axis_index("seq")
@@ -104,6 +102,8 @@
     peers = range(1, devices)
     wide = UNITS * rows
     steps = blocks * group // UNITS
+    late = late_peers(devices)
+    stages = stage_list(devices)
 
     def peer(k):
         return me ^ k
@@ -155,27 +155,44 @@
 
     def need_copy(k):
         return pltpu.make_async_remote_copy(
-            need_out, need_in.at[k], send_need.at[k], recv_need.at[k], device_id={"seq": peer(k)}
+            need_out, need_in.at[k], send_sem.at[0], recv_need.at[k - 1], device_id={"seq": peer(k)}
         )
 
     def chunk_copy(k):
         return pltpu.make_async_remote_copy(
             chunk_out.at[lax.rem(peer(k), CHUNKS)],
             chunk_in.at[me],
-            send_chunk.at[k],
-            recv_chunk.at[k],
+            send_sem.at[1],
+            recv_sem.at[0],
             device_id={"seq": peer(k)},
         )
 
+    alike = range(2, devices, 2)
+
     def reg_copy(k):
         return pltpu.make_async_remote_copy(
-            reg_out, reg_in.at[me], send_reg.at[k], recv_reg.at[k], device_id={"seq": peer(k)}
+            reg_out, reg_in.at[me], send_sem.at[2], recv_sem.at[1], device_id={"seq": peer(k)}
         )
 
-    def x_copy(k, g):
+    def pass_copy(k):
         return pltpu.make_async_remote_copy(
-            x_out.at[k, g], x_in.at[k, g], send_x.at[k, g], recv_x.at[k, g], device_id={"seq": peer(k)}
+            reg_in.at[peer(k)], reg_in.at[peer(k)], send_sem.at[3], recv_sem.at[2], device_id={"seq": peer(1)}
         )
+
+    def x_copy(k, g, part):
+        span = pl.ds(part * rows, rows if k in late else 2 * rows)
+        n = [k in stage for stage in stages].index(True) + part
+        return pltpu.make_async_remote_copy(
+            x_out.at[k, g, span], x_in.at[k, g, span], send_sem.at[4], recv_x.at[n, g], device_id={"seq": peer(k)}
+        )
+
+    def total(ref, kind, received):
+        return pltpu.make_async_remote_copy(ref, ref, send_sem.at[kind], received, device_id={"seq": peer(1)})
+
+    def arrive(stage, g, part):
+        span = pl.ds(part * rows, rows if stage == late else 2 * rows)
+        ref = x_in.at[pl.ds(min(stage), len(stage)), g, span]
+        total(ref, 4, recv_x.at[stages.index(stage) + part, g]).wait_recv()
 
     order = list(reversed(peers))
     for k in order:
@@ -190,36 +207,40 @@
             vt_own[b, g, :HEAD_SIZE] = v_all[b, :, column].T
             vt_own[b, g, HEAD_SIZE:] = jnp.ones((SUMS, rows), bf)
 
-    stages = stage_list(devices)
-
-    for k in peers:
+    picks = {}
+
+    def fill(k, g):
+        columns = pl.ds(g * HEAD_SIZE, HEAD_SIZE)
+        x_out[k, g, :rows] = k_all[picks[k], :, columns]
+        x_out[k, g, rows:] = vt_own[picks[k], g, :HEAD_SIZE]
+
+    def answer(k):
         need_copy(k).wait_recv()
-    picks = {}
-    for k in peers:
         row = need_in[k]
         picks[k] = jnp.sum(jnp.where(lane[:1] == me, row[:1], 0))
-
-    def fill(k, g):
-        columns = slice(g * HEAD_SIZE, (g + 1) * HEAD_SIZE)
-        x_out[k, g, :rows] = k_all[picks[k], :, columns]
-        x_out[k, g, rows:] = vt_own[picks[k], g, :HEAD_SIZE]
-
-    for group_of in stages:
-        for k in group_of:
-            fill(k, 0)
-            x_copy(k, 0).start()
-    for k in peers:
-        chunk_copy(k).wait_recv()
+        fill(k, 0)
+        if k not in late:
+            x_copy(k, 0, 0).start()
+
+    everyone = [k for stage in stages for k in stage]
+    for k in everyone[:3]:
+        answer(k)
+    total(chunk_in.at[pl.ds(0, devices - 1)], 1, recv_sem.at[0]).wait_recv()
     mine = chunk_in[owner_ref[0]]
     reg_out[...] = mine
     reg_in[me] = mine
-    for k in order:
+    for k in reversed(alike):
         reg_copy(k).start()
-    for g in range(1, KEY_VALUE_HEADS):
-        for group_of in stages:
-            for k in group_of:
-                fill(k, g)
-                x_copy(k, g).start()
+    pass_copy(0).start()
+    for k in everyone[3:]:
+        answer(k)
+
+    def send(g):
+        for k in everyone:
+            fill(k, g)
+            x_copy(k, g, 0).start()
+        for k in late:
+            x_copy(k, g, 1).start()
 
     for k in peers:
         source = peer(k)
@@ -238,14 +259,29 @@
     nt = (((1,), (1,)), ((), ()))
 
     def own_step(b, carry):
+        @pl.when(b == 1)
+        def _():
+            for part in range(2):
+                for k in late:
+                    x_copy(k, 0, part).start()
+
+        @pl.when(b == blocks - 1)
+        def _():
+            send(1)
+
+        @pl.when(b == blocks - 1)
+        def _():
+            total(reg_in.at[pl.ds(0, len(alike))], 2, recv_sem.at[1]).wait_recv()
+            for k in alike:
+                pass_copy(k).start()
+
         q_copy(b).wait()
         row_span = pl.ds(pl.multiple_of(b * rows, rows), rows)
         place = pl.ds(pl.multiple_of(b * group * rows, rows), group * rows)
         mask = jnp.concatenate([own_mask[b]] * group, axis=1)
 
         def scored(g):
-            high, low = split(k_all[b, :, g * HEAD_SIZE : (g + 1) * HEAD_SIZE])
-            both = jnp.concatenate([high, low], axis=1)
+            own_keys = k_all[b, :, g * HEAD_SIZE : (g + 1) * HEAD_SIZE]
             query = jnp.concatenate(
                 [
                     q_all[row_span, (g * group + h) * HEAD_SIZE : (g * group + h + 1) * HEAD_SIZE]
@@ -253,8 +289,7 @@
                 ],
                 axis=0,
             )
-            query = jnp.concatenate([query, query], axis=1)
-            return lax.dot_general(both, query, nt, preferred_element_type=f32) + mask
+            return lax.dot_general(own_keys, query, nt, preferred_element_type=f32) * score_gain + mask
 
         ahead = scored(0)
         for g in range(KEY_VALUE_HEADS):
@@ -269,21 +304,31 @@
         return carry
 
     lax.fori_loop(0, blocks, own_step, 0)
-
-    for k in peers:
-        reg_copy(k).wait_recv()
+    total(reg_in.at[pl.ds(0, devices // 2)], 3, recv_sem.at[2]).wait_recv()
 
     half = CHUNKS // 2
 
     def far_stage(g, stage, first, last):
-        total = len(stage) * rows + (REG if first else 0)
-        for k in stage:
-            x_copy(k, g).wait_recv()
+        size_all = len(stage) * rows + (REG if first else 0)
+        apart = stage == late
+        arrive(stage, g, 0)
+        if first:
+
+            @pl.when(g < KEY_VALUE_HEADS - 2)
+            def _():
+                send(g + 2)
+
         for n, k in enumerate(stage):
             high, low = split(x_in[k, g, :rows])
             kk[n * rows : (n + 1) * rows, :HEAD_SIZE] = high
             kk[n * rows : (n + 1) * rows, HEAD_SIZE:] = low
-            vt[:HEAD_SIZE, n * rows : (n + 1) * rows] = x_in[k, g, rows:]
+
+        def load_values():
+            for n, k in enumerate(stage):
+                vt[:HEAD_SIZE, n * rows : (n + 1) * rows] = x_in[k, g, rows:]
+
+        if not apart:
+            load_values()
         if first:
             column = pl.ds(pl.multiple_of(g * HEAD_SIZE, HEAD_SIZE), HEAD_SIZE)
             begin = len(stage) * rows
@@ -309,67 +354,82 @@
             place = place_of(j)
             query = jnp.concatenate([q_all[unit(j, n)] for n in range(UNITS)], axis=0)
             query = jnp.concatenate([query, query], axis=1)
-            scores = lax.dot_general(kk[:total], query, nt, preferred_element_type=f32)
-            s_ref[:total] = scores
+            scores = lax.dot_general(kk[:size_all], query, nt, preferred_element_type=f32)
+            s_ref[:size_all] = scores
             best = top[g, :, place]
             for begin, size, k in pieces:
                 block = jnp.max(scores[begin : begin + size].reshape(size // 8, 8, wide), axis=0)
                 best = jnp.maximum(best, block if k is None else block + shown[k, :, place])
             m_ref[...] = jnp.broadcast_to(jnp.max(best, axis=0, keepdims=True), (8, wide))
 
-        def merge(j, s_ref, m_ref):
+        def weigh(j, s_ref, best, chosen):
+            parts = []
+            for begin, size, k in chosen:
+                shift = -best if k is None else shown[k, :, place_of(j)] - best
+                block = s_ref[begin : begin + size].reshape(size // 8, 8, wide)
+                parts.append(jnp.exp2(block + shift[None]).reshape(size, wide).astype(bf))
+            return jnp.concatenate(parts, axis=0)
+
+        def finish(j, product, best):
             place = place_of(j)
-            before = top[g, :, place]
-            best = m_ref[...]
-            product = None
-            for c in range(0, len(pieces), 2):
-                parts = []
-                for begin, size, k in pieces[c : c + 2]:
-                    shift = -best if k is None else shown[k, :, place] - best
-                    block = s_ref[begin : begin + size].reshape(size // 8, 8, wide)
-                    parts.append(jnp.exp2(block + shift[None]).reshape(size, wide).astype(bf))
-                begin = pieces[c][0]
-                weights = jnp.concatenate(parts, axis=0)
-                more = jnp.dot(vt[:, begin : begin + weights.shape[0]], weights, preferred_element_type=f32)
-                product = more if product is None else product + more
-            product = product[: HEAD_SIZE + 8]
-            scale = jnp.exp2(before - best)
-            product = product.reshape(HEAD_SIZE // 8 + 1, 8, wide)
+            scale = jnp.exp2(top[g, :, place] - best)
+            product = product[: HEAD_SIZE + 8].reshape(HEAD_SIZE // 8 + 1, 8, wide)
             product = product + acc[g, :, place].reshape(HEAD_SIZE // 8 + 1, 8, wide) * scale[None]
             if last:
                 share = 1.0 / product[HEAD_SIZE // 8]
                 merged = (product[: HEAD_SIZE // 8] * share[None]).reshape(HEAD_SIZE, wide).astype(bf)
                 for n in range(UNITS):
-                    out_ref[unit(j, n)] = merged[:, n * rows : (n + 1) * rows].T
+                    out_all[unit(j, n)] = merged[:, n * rows : (n + 1) * rows].T
             else:
                 acc[g, :, place] = product.reshape(HEAD_SIZE + 8, wide)
                 top[g, :, place] = best
 
+        def merge(j, s_ref, m_ref):
+            best = m_ref[...]
+            product = None
+            for c in range(0, len(pieces), 2):
+                begin = pieces[c][0]
+                weights = weigh(j, s_ref, best, pieces[c : c + 2])
+                more = jnp.dot(vt[:, begin : begin + weights.shape[0]], weights, preferred_element_type=f32)
+                product = more if product is None else product + more
+            finish(j, product, best)
+
+        def keep(j, s_ref, m_ref):
+            best = m_ref[...]
+            held[:, place_of(j)] = weigh(j, s_ref, best, pieces)
+            held_top[:, place_of(j)] = best
+
         score(0, s_a, m_a)
-
         buffers = ((s_a, m_a), (s_b, m_b))
         for j in range(steps):
             if j + 1 < steps:
                 score(j + 1, *buffers[(j + 1) % 2])
-            merge(j, *buffers[j % 2])
-
-    def far_group(g, carry, plan):
-        for stage in plan:
-            far_stage(g, stage, stage == plan[0], stage == plan[-1])
+            (keep if apart else merge)(j, *buffers[j % 2])
+        if apart:
+            arrive(stage, g, 1)
+            load_values()
+            for j in range(steps):
+                product = jnp.dot(vt[:, :size_all], held[:, place_of(j)], preferred_element_type=f32)
+                finish(j, product, held_top[:, place_of(j)])
+
+    def out_copy(g):
+        span = pl.ds(pl.multiple_of(g * group * HEAD_SIZE, HEAD_SIZE), group * HEAD_SIZE)
+        return pltpu.make_async_copy(out_all.at[:, span], out_ref.at[:, span], out_sem.at[0])
+
+    def far_group(g, carry):
+        for stage in stages:
+            far_stage(g, stage, stage == stages[0], stage == stages[-1])
+        out_copy(g).start()
         return carry
 
-    ends = last_list(devices)
-    same = KEY_VALUE_HEADS - (ends != stages)
-    lax.fori_loop(0, same, functools.partial(far_group, plan=stages), 0)
-    for g in range(same, KEY_VALUE_HEADS):
-        far_group(g, 0, ends)
-
-    for k in peers:
-        need_copy(k).wait_send()
-        chunk_copy(k).wait_send()
-        reg_copy(k).wait_send()
-        for g in range(KEY_VALUE_HEADS):
-            x_copy(k, g).wait_send()
+    lax.fori_loop(0, KEY_VALUE_HEADS, far_group, 0)
+
+    pltpu.make_async_copy(out_all, out_ref, out_sem.at[0]).wait()
+    total(need_in.at[pl.ds(0, devices - 1)], 0, recv_sem.at[0]).wait_send()
+    total(chunk_in.at[pl.ds(0, devices - 1)], 1, recv_sem.at[0]).wait_send()
+    total(reg_in.at[pl.ds(0, len(alike))], 2, recv_sem.at[1]).wait_send()
+    total(reg_in.at[pl.ds(0, devices // 2)], 3, recv_sem.at[2]).wait_send()
+    total(x_out.at[pl.ds(1, devices - 1)], 4, recv_sem.at[0]).wait_send()
 
 
 def per_device(queries, keys, values, reg_owner, block_lists, list_counts, image_blocks):
@@ -388,7 +448,7 @@
         functools.partial(kernel, devices),
         out_shape=jax.ShapeDtypeStruct((tokens, width), bf),
         in_specs=[anywhere] * 7,
-        out_specs=pl.BlockSpec(memory_space=pltpu.VMEM),
+        out_specs=pl.BlockSpec(memory_space=pl.ANY),
         scratch_shapes=[
             pltpu.SMEM((blocks, slots), jnp.int32),
             pltpu.SMEM((blocks,), jnp.int32),
@@ -416,17 +476,17 @@
             pltpu.VMEM((far, UNITS * rows), f32),
             pltpu.VMEM((8, UNITS * rows), f32),
             pltpu.VMEM((8, UNITS * rows), f32),
+            pltpu.VMEM((max(1, len(late_peers(devices))) * rows, spread), bf),
+            pltpu.VMEM((8, spread), f32),
+            pltpu.VMEM((tokens, width), bf),
+            dma((1,)),
             dma((4,)),
             dma((2,)),
             dma((blocks,)),
-            dma((devices,)),
-            dma((devices,)),
-            dma((devices,)),
-            dma((devices,)),
-            dma((devices,)),
-            dma((devices,)),
-            dma((devices, KEY_VALUE_HEADS)),
-            dma((devices, KEY_VALUE_HEADS)),
+            dma((5,)),
+            dma((devices - 1,)),
+            dma((3,)),
+            dma((len(stage_list(devices)) + (1 if late_peers(devices) else 0), KEY_VALUE_HEADS)),
         ],
         compiler_params=pltpu.CompilerParams(
             collective_id=0, has_side_effects=True, vmem_limit_bytes=42 * 1024 * 1024 + devices * kv_width * rows * 4

time: 40.7 us -> 37.6 us (0.924)
  Pallas kernels: 38.1 us -> 34.9 us
    pallas_call x1, Pallas kernels: 38.1 us -> 34.9 us  [per_device(): pl.pallas_call(functools.partial(kernel, devices), out_shape=jax.ShapeDty...]
where the time goes in v3:
time: 37.6 us; the launch traced here: 37.4 us
  Pallas kernels  34.9 us (93%)
  local copies, waits for them, and re-layouts  1.84 us (5%)
  between operations  0.66 us (2%)
    pallas_call x1, Pallas kernels, per_device(): pl.pallas_call(functools.partial(kernel, devices), out_shape=jax.ShapeDty...  34.9 us
    unnamed x1, local copies, waits for them, and re-layouts  1.84 us

profile of v3, /device:TPU:1, one launch (start us, length us, event | category | flops | bytes accessed | tf_op | source)
XLA Modules:
  0.0 37.4 jit_solution(13630493791806674)
XLA Ops:
  0.7 34.9 %shard_map.73 = bf16[512,3584]{1,0:T(8,128)(2,1)S(1)} custom-call(s32[4,8]{1,0:T(4,128)} %bitcast.11, s32[4]{0:T(128)} %bitcast.12, s32[4]{0:T(128)} %bitcast.13, s32[1]{0:T(128)S(6)} %copy.9.owner_hbm, bf16[512,3584]{1,0:T(8,128)(2,1)} %bitcast.8, bf16[4,128,512]{2,1,0:T(8,128)(2,1)} %bitcast.9, bf16[4,128,512]{2,1,0:T(8,128)(2,1)} %bitcast.10), custom_call_target="tpu_custom_call" | custom-call | tf_op jit(solution)/shard_map/pallas_call | solution.py:447
  35.5 1.8 %copy.10 = bf16[1,512,3584]{2,1,0:T(8,128)(2,1)} copy(bf16[1,512,3584]{2,1,0:T(8,128)(2,1)S(1)} %bitcast.7) | data formatting | bytes 7340032
